TPU v7x, 256 devices: a 8x8x2 block of a 8x8x16 slice. The times are simulated.
256 devices in a mesh: groups: 2 (over z), dap: 128 (over x, y, core).
Axes of the slice: x: 8, y: 8, z: 2, core: 2. Of those that a mesh axis runs over, the one named last changes fastest.
The devices are a block of a 8x8x16 slice.
Arguments:
- homolog_tensor: bfloat16 [1024, 256, 256], P(('groups', 'dap')), parts along dimension 0, may hold values from -1 to 1
- couple_tensor: bfloat16 [512, 256, 128], P(('groups', 'dap')), parts along dimension 0, may hold values from -6 to 6
- horizontal_drop_filter: int32 [512, 256], P('groups'), parts along dimension 0, may hold values 0 or 1
- couple_offset_matrix: bfloat16 [128, 8], replicated, may hold values from -0.29882812 to 0.29882812
- horizontal_attend_matrix: bfloat16 [256, 1024], replicated, may hold values from -0.375 to 0.375
- horizontal_exit_matrix: bfloat16 [256, 256], replicated, may hold values from -0.375 to 0.375
- vertical_attend_matrix: bfloat16 [256, 1024], replicated, may hold values from -0.375 to 0.375
- vertical_exit_matrix: bfloat16 [256, 256], replicated, may hold values from -0.375 to 0.375
- averaged_product_flanks: bfloat16 [256, 64], replicated, may hold values from -0.375 to 0.375
- averaged_product_exit: bfloat16 [1024, 128], replicated, may hold values from -1 to 1
Outputs:
- alignment_output: bfloat16 [1024, 256, 256], P('groups', 'dap'), parts along dimension 0
- pair_output_state: bfloat16 [512, 256, 128], P(('groups', 'dap')), parts along dimension 0
There are 2 independent parts, one for each index of `groups`. A program takes and returns all parts, laid end to end along the dimension named above; an argument that names none is the same for every part. Nothing has to cross between parts.
All inputs are finite; a program needn't handle non-finite values.
Results may differ from a plain program's by a relative error of at most 0.012.
Values may be sent and summed in bfloat16 or wider, within the bound.
A program may use at most 64 MiB of HBM per device.

v0:
```python
import jax
import jax.numpy as jnp
from jax import lax
from jax.sharding import Mesh
from jax.sharding import PartitionSpec as P

HEAD_NUMBER = 8
HEAD_WIDTH = 32
FACTOR_FEATURES = 32
DAP = ("dap_0", "dap_1", "dap_2")
GROUPS_DAP = ("groups", "dap_0", "dap_1", "dap_2")


def joined_along(tiles, dim):
    tiles = jnp.moveaxis(tiles, 0, dim)
    dims = tiles.shape
    return tiles.reshape(*dims[:dim], dims[dim] * dims[dim + 1], *dims[dim + 2 :])


def stacked_from(shard, axes, order):
    tiles = shard[None]
    for k in order:
        tiles = lax.all_gather(tiles, axes[k], axis=0, tiled=True)
    carried = [lax.axis_size(axes[k]) for k in reversed(order)]
    tiles = tiles.reshape(*carried, *shard.shape)
    turned = sorted(range(len(order)), key=lambda place: order[len(order) - 1 - place])
    return tiles.transpose(*turned, *range(len(order), tiles.ndim)).reshape(-1, *shard.shape)


def gather_axes(shard, axes, order, dim):
    return joined_along(stacked_from(shard, axes, order), dim)


def standardise_features(values):
    values = values.astype(jnp.float32)
    center = values - jnp.mean(values, axis=-1, keepdims=True)
    spread = jnp.mean(center * center, axis=-1, keepdims=True)
    return center * lax.rsqrt(spread + 1e-05)


def attend(normed, w_qkvg, w_out, bias):
    batch, length = (normed.shape[0], normed.shape[1])
    proj = jnp.einsum("blc,cf->blf", normed, w_qkvg, preferred_element_type=jnp.float32)
    proj = proj.reshape(batch, length, 4, HEAD_NUMBER, HEAD_WIDTH)
    query = (proj[:, :, 0] * HEAD_WIDTH ** (-0.5)).astype(jnp.bfloat16)
    keys = proj[:, :, 1].astype(jnp.bfloat16)
    values = proj[:, :, 2].astype(jnp.bfloat16)
    gate = proj[:, :, 3]
    if bias is None:
        bias = jnp.zeros((HEAD_NUMBER, length, length), jnp.bfloat16)

    def one_head(items):
        qh, kh, vh, bh = items
        scores = jnp.einsum("bid,bjd->bij", qh, kh, preferred_element_type=jnp.float32)
        scores = scores + bh.astype(jnp.float32)[None]
        weights = jax.nn.softmax(scores, axis=-1).astype(jnp.bfloat16)
        return jnp.einsum("bij,bjd->bid", weights, vh, preferred_element_type=jnp.float32)

    heads = lax.map(
        one_head,
        (jnp.moveaxis(query, 2, 0), jnp.moveaxis(keys, 2, 0), jnp.moveaxis(values, 2, 0), bias),
    )
    heads = jnp.moveaxis(heads, 0, 2)
    gated = (
        (jax.nn.sigmoid(gate) * heads)
        .astype(jnp.bfloat16)
        .reshape(batch, length, HEAD_NUMBER * HEAD_WIDTH)
    )
    return jnp.einsum("blk,kc->blc", gated, w_out, preferred_element_type=jnp.float32)


def shards(
    homolog_tensor,
    couple_tensor,
    horizontal_drop_filter,
    couple_offset_matrix,
    horizontal_attend_matrix,
    horizontal_exit_matrix,
    vertical_attend_matrix,
    vertical_exit_matrix,
    averaged_product_flanks,
    averaged_product_exit,
):
    normed_pair = standardise_features(couple_tensor).astype(jnp.bfloat16)
    own_bias = jnp.einsum(
        "ijz,zh->hij", normed_pair, couple_offset_matrix, preferred_element_type=jnp.float32
    ).astype(jnp.bfloat16)
    bias = gather_axes(own_bias, DAP, (0, 1, 2), 1)
    starting_answer = standardise_features(homolog_tensor).astype(jnp.bfloat16)
    perform_refresh = attend(
        starting_answer, horizontal_attend_matrix, horizontal_exit_matrix, bias
    )
    homolog_later = (
        homolog_tensor.astype(jnp.float32)
        + horizontal_drop_filter.astype(jnp.float32) * (1.0 / 0.9) * perform_refresh
    ).astype(jnp.bfloat16)
    incoming_blocks = lax.all_to_all(homolog_later, DAP, split_axis=1, concat_axis=0, tiled=True)
    column_layout = jnp.swapaxes(incoming_blocks, 0, 1)
    perform_refresh = attend(
        standardise_features(column_layout).astype(jnp.bfloat16),
        vertical_attend_matrix,
        vertical_exit_matrix,
        None,
    )
    alignment_output = jnp.swapaxes(
        (column_layout.astype(jnp.float32) + perform_refresh).astype(jnp.bfloat16), 0, 1
    )
    final_result = standardise_features(alignment_output).astype(jnp.bfloat16)
    factors = jnp.einsum(
        "sic,cf->sif", final_result, averaged_product_flanks, preferred_element_type=jnp.float32
    )
    left = factors[..., :FACTOR_FEATURES].astype(jnp.bfloat16)
    right = factors[..., FACTOR_FEATURES:].astype(jnp.bfloat16)
    total = left.shape[0]
    own_rows = left.shape[1]
    piece = lax.all_gather(right, DAP, axis=1, tiled=True)
    outer = jnp.einsum("sic,sjd->ijcd", left, piece, preferred_element_type=jnp.float32) / total
    outer = outer.astype(jnp.bfloat16).reshape(
        own_rows, piece.shape[1], FACTOR_FEATURES * FACTOR_FEATURES
    )
    change = jnp.einsum(
        "ijk,kz->ijz", outer, averaged_product_exit, preferred_element_type=jnp.float32
    )
    pair_output_state = (couple_tensor.astype(jnp.float32) + change).astype(jnp.bfloat16)
    return (alignment_output, pair_output_state)


def solution(mesh):
    torus = Mesh(
        mesh.devices.reshape(mesh.shape["groups"], 8, 8, 2), ("groups", "dap_0", "dap_1", "dap_2")
    )
    return jax.shard_map(
        shards,
        mesh=torus,
        in_specs=(
            P(GROUPS_DAP, None, None),
            P(GROUPS_DAP, None, None),
            P("groups", None),
            P(),
            P(),
            P(),
            P(),
            P(),
            P(),
            P(),
        ),
        out_specs=(P("groups", DAP, None), P(GROUPS_DAP, None, None)),
        check_vma=False,
    )
```

profile of v0, /device:TPU:513, one launch (start us, length us, event | category | flops | bytes accessed | tf_op | source)
XLA Modules:
  0.0 365.0 jit_solution(12928804633516290471)
XLA Ops:
  10.7 20.9 %all-gather = bf16[64,2,256]{2,0,1:T(8,128)(2,1)S(1)} all-gather(bf16[8,2,256]{2,0,1:T(8,128)(2,1)S(1)} %fusion.37), channel_id=2, replica_groups=mesh['groups'=2,'dap_0'=8,'dap_1'=8,'dap_2'=2] {'dap_0'}, dimensions={0}, use_global_device_ids=true | all-gather | bytes 73728 | tf_op jit(solution)/shard_map/all_gather | solution.py:23
  31.7 30.9 %all_gather.13 = bf16[64,8,2,256]{3,1,0,2:T(8,128)(2,1)} all-gather(bf16[8,8,2,256]{3,1,0,2:T(8,128)(2,1)S(1)} %bitcast.194), channel_id=1, replica_groups=mesh['groups'=2,'dap_0'=8,'dap_1'=8,'dap_2'=2] {'dap_1'}, dimensions={0}, use_global_device_ids=true | all-gather | bytes 589824 | tf_op jit(solution)/shard_map/all_gather | solution.py:23
  65.3 2.0 fusion.59
  71.5 27.3 %all-gather.4.cloned.1.call-done = bf16[128,8,2,256]{3,1,0,2:T(8,128)(2,1)} async-done(((bf16[64,8,2,256]{3,1,0,2:T(8,128)(2,1)}), bf16[128,8,2,256]{3,1,0,2:T(8,128)(2,1)}) %all-gather.4.cloned.1.call-update) | async-done | bytes 1048592 | tf_op jit(solution)/shard_map/all_gather | solution.py:23
  101.0 36.0 %while.20 = (s32[]{:T(128)}, f32[8,4,256,32]{2,3,0,1:T(8,128)}, bf16[8,4,256,32]{2,3,0,1:T(8,128)(2,1)}, bf16[8,4,256,32]{2,3,0,1:T(8,128)(2,1)}, bf16[8,256,256...) while((s32[]{:T(128)}, f32[8,4,256,32]{2,3,0,1:T(8,128)}, ...), condition=%wide.region_7.8_spmd, body=%wide.region_4.7_spmd.sunk | while | flops 52233728 | bytes 4533337 | solution.py:59
  103.7 1.9 fusion.105
  108.2 1.9 fusion.105
  112.6 1.9 fusion.105
  117.1 1.8 fusion.105
  121.6 1.8 fusion.105
  126.1 1.8 fusion.105
  130.6 1.8 fusion.105
  135.1 1.9 fusion.105
  136.9 1.8 fusion.54
  141.3 14.5 %all-to-all-start = ((bf16[4,256,256]{2,0,1:T(4,128)(2,1)}), bf16[4,256,256]{2,0,1:T(4,128)(2,1)S(1)}, u32[]{:S(2)}, u32[]{:S(2)}) async-start(bf16[4,256,256]{2,0,1:T(4,128)(2,1)} %copy.59), calls=%async_computation | async-start | bytes 1048576 | tf_op jit(solution)/shard_map/all_to_all | solution.py:97
  156.1 18.9 %all-to-all-done = bf16[4,256,256]{2,0,1:T(4,128)(2,1)S(1)} async-done(((bf16[4,256,256]{2,0,1:T(4,128)(2,1)}), bf16[4,256,256]{2,0,1:T(4,128)(2,1)S(1)}, u32[]{:S(2)}, u32[]{:S(2)}) %all-to-all-start) | async-done | bytes 524320 | tf_op jit(solution)/shard_map/all_to_all | solution.py:97
  177.6 1.8 multiply_convert_fusion.1
  180.3 1.8 copy-done.1
  184.5 2.1 slice_bitcast_fusion
  186.6 73.0 %while.21 = (s32[]{:T(128)}, f32[8,2,512,32]{2,3,0,1:T(8,128)}, bf16[8,2,512,32]{2,3,0,1:T(8,128)(2,1)S(1)}, bf16[8,2,512,32]{2,3,0,1:T(8,128)(2,1)}, bf16[8,2,512,32]{2,3,0,1:T(8,128)(2,1)S(1)}, /*index=5*/s32[]{:T(128)}) while((s32[]{:T(128)}, f32[8,2,512,32]{2,3,0,1:T(8,128)}, bf16[8,2,512,32]{2,3,0,1:T(8,128)(2,1)S(1)}, ...), condition=%wide.region_13.14_spmd, body=%wide.region_10.13_spmd.sunk | while | flops 67108864 | bytes 1507417 | solution.py:59
  190.1 3.8 %dot_general.47 = f32[2,512,32]{2,1,0:T(8,128)} custom-call(bf16[2,512,32]{2,1,0:T(8,128)(2,1)} %bitcast.177, bf16[2,512,32]{2,1,0:T(8,128)(2,1)} %bitcast.176, bf16[2,512,32]{2,1,0:T(8,128)(2,1)} %bitcast.178), custom_call_target="tpu_custom_call" | custom-call | flops 67108864 | bytes 196608 | tf_op jit(solution)/shard_map/while/body/eval_jaxpr/bij,bjd->bid/dot_general | solution.py:57
  199.2 3.8 %dot_general.47 = f32[2,512,32]{2,1,0:T(8,128)} custom-call(bf16[2,512,32]{2,1,0:T(8,128)(2,1)} %bitcast.177, bf16[2,512,32]{2,1,0:T(8,128)(2,1)} %bitcast.176, bf16[2,512,32]{2,1,0:T(8,128)(2,1)} %bitcast.178), custom_call_target="tpu_custom_call" | custom-call | flops 67108864 | bytes 196608 | tf_op jit(solution)/shard_map/while/body/eval_jaxpr/bij,bjd->bid/dot_general | solution.py:57
  208.3 3.8 %dot_general.47 = f32[2,512,32]{2,1,0:T(8,128)} custom-call(bf16[2,512,32]{2,1,0:T(8,128)(2,1)} %bitcast.177, bf16[2,512,32]{2,1,0:T(8,128)(2,1)} %bitcast.176, bf16[2,512,32]{2,1,0:T(8,128)(2,1)} %bitcast.178), custom_call_target="tpu_custom_call" | custom-call | flops 67108864 | bytes 196608 | tf_op jit(solution)/shard_map/while/body/eval_jaxpr/bij,bjd->bid/dot_general | solution.py:57
  217.4 3.8 %dot_general.47 = f32[2,512,32]{2,1,0:T(8,128)} custom-call(bf16[2,512,32]{2,1,0:T(8,128)(2,1)} %bitcast.177, bf16[2,512,32]{2,1,0:T(8,128)(2,1)} %bitcast.176, bf16[2,512,32]{2,1,0:T(8,128)(2,1)} %bitcast.178), custom_call_target="tpu_custom_call" | custom-call | flops 67108864 | bytes 196608 | tf_op jit(solution)/shard_map/while/body/eval_jaxpr/bij,bjd->bid/dot_general | solution.py:57
  226.6 3.8 %dot_general.47 = f32[2,512,32]{2,1,0:T(8,128)} custom-call(bf16[2,512,32]{2,1,0:T(8,128)(2,1)} %bitcast.177, bf16[2,512,32]{2,1,0:T(8,128)(2,1)} %bitcast.176, bf16[2,512,32]{2,1,0:T(8,128)(2,1)} %bitcast.178), custom_call_target="tpu_custom_call" | custom-call | flops 67108864 | bytes 196608 | tf_op jit(solution)/shard_map/while/body/eval_jaxpr/bij,bjd->bid/dot_general | solution.py:57
  235.7 3.8 %dot_general.47 = f32[2,512,32]{2,1,0:T(8,128)} custom-call(bf16[2,512,32]{2,1,0:T(8,128)(2,1)} %bitcast.177, bf16[2,512,32]{2,1,0:T(8,128)(2,1)} %bitcast.176, bf16[2,512,32]{2,1,0:T(8,128)(2,1)} %bitcast.178), custom_call_target="tpu_custom_call" | custom-call | flops 67108864 | bytes 196608 | tf_op jit(solution)/shard_map/while/body/eval_jaxpr/bij,bjd->bid/dot_general | solution.py:57
  244.8 3.8 %dot_general.47 = f32[2,512,32]{2,1,0:T(8,128)} custom-call(bf16[2,512,32]{2,1,0:T(8,128)(2,1)} %bitcast.177, bf16[2,512,32]{2,1,0:T(8,128)(2,1)} %bitcast.176, bf16[2,512,32]{2,1,0:T(8,128)(2,1)} %bitcast.178), custom_call_target="tpu_custom_call" | custom-call | flops 67108864 | bytes 196608 | tf_op jit(solution)/shard_map/while/body/eval_jaxpr/bij,bjd->bid/dot_general | solution.py:57
  253.9 3.8 %dot_general.47 = f32[2,512,32]{2,1,0:T(8,128)} custom-call(bf16[2,512,32]{2,1,0:T(8,128)(2,1)} %bitcast.177, bf16[2,512,32]{2,1,0:T(8,128)(2,1)} %bitcast.176, bf16[2,512,32]{2,1,0:T(8,128)(2,1)} %bitcast.178), custom_call_target="tpu_custom_call" | custom-call | flops 67108864 | bytes 196608 | tf_op jit(solution)/shard_map/while/body/eval_jaxpr/bij,bjd->bid/dot_general | solution.py:57
  259.7 1.8 fusion.55
  264.1 77.3 %all-gather.6.cloned.1.call-done = bf16[512,256,32]{0,2,1:T(8,128)(2,1)} async-done(((bf16[512,2,32]{0,2,1:T(8,128)(2,1)}), bf16[512,256,32]{0,2,1:T(8,128)(2,1)}) %all-gather.6.cloned.1.call-update) | async-done | bytes 8388624 | tf_op jit(solution)/shard_map/all_gather | solution.py:116
  341.4 9.4 %fusion.26 = bf16[2,256,32,32]{2,3,0,1:T(8,128)(2,1)} fusion(bf16[512,256,32]{0,2,1:T(8,128)(2,1)} %all-gather.6.cloned.1.call-done, bf16[512,2,64]{0,2,1:T(8,128)(2,1)S(1)} %convolution_convert_fusion), kind=kOutput, calls=%fused_computation.30 | convolution fusion | flops 537919488 | bytes 9502720 | tf_op jit(solution)/shard_map/sic,sjd->ijcd/dot_general | solution.py:117
  350.8 6.2 %copy.71 = bf16[2,256,32,32]{1,3,2,0:T(8,128)(2,1)S(1)} copy(bf16[2,256,32,32]{2,3,0,1:T(8,128)(2,1)} %fusion.26) | data formatting | bytes 2097152 | tf_op jit(solution)/shard_map/convert_element_type | solution.py:118
  (141 shorter events, 88.3 us)
Async XLA Ops:
  7.2 58.2 %copy-start = (bf16[256,1024]{1,0:T(8,128)(2,1)S(1)}, bf16[256,1024]{1,0:T(8,128)(2,1)}, u32[]{:S(2)}) copy-start(bf16[256,1024]{1,0:T(8,128)(2,1)} %param.18) | copy-start | bytes 1572868
  7.2 91.6 %all-gather.4.cloned.1.call-start = ((), (), s32[]{:S(2)}) async-start(), calls=%async_computation.1 | async-start | bytes 1572864 | tf_op jit(solution)/shard_map/all_gather | solution.py:23
  67.4 3.0 copy-start.2
  67.4 1.1 copy-start.6
  100.9 37.8 %copy-start.3 = (bf16[4,256,256]{2,1,0:T(8,128)(2,1)S(1)}, bf16[4,256,256]{2,1,0:T(8,128)(2,1)}, u32[]{:S(2)}) copy-start(bf16[4,256,256]{2,1,0:T(8,128)(2,1)} %param.14) | copy-start | bytes 1572868
  101.0 37.8 %copy-start.9 = (bf16[256,256]{1,0:T(8,128)(2,1)S(1)}, bf16[256,256]{1,0:T(8,128)(2,1)}, u32[]{:S(2)}) copy-start(bf16[256,256]{1,0:T(8,128)(2,1)} %param.19) | copy-start | bytes 393220
  141.3 38.1 %copy-start.5 = (bf16[256,1024]{1,0:T(8,128)(2,1)S(1)}, bf16[256,1024]{1,0:T(8,128)(2,1)}, u32[]{:S(2)}) copy-start(bf16[256,1024]{1,0:T(8,128)(2,1)} %param.20) | copy-start | bytes 1572868
  141.3 33.6 %all-to-all-start = ((bf16[4,256,256]{2,0,1:T(4,128)(2,1)}), bf16[4,256,256]{2,0,1:T(4,128)(2,1)S(1)}, u32[]{:S(2)}, u32[]{:S(2)}) async-start(bf16[4,256,256]{2,0,1:T(4,128)(2,1)} %copy.59), calls=%async_computation | async-start | bytes 1048576 | tf_op jit(solution)/shard_map/all_to_all | solution.py:97
  155.8 185.6 %all-gather.6.cloned.1.call-start = ((), (), s32[]{:S(2)}) async-start(), calls=%async_computation.2 | async-start | bytes 8454144 | tf_op jit(solution)/shard_map/all_gather | solution.py:116
  180.1 1.9 copy-start.1
  186.6 74.9 %copy-start.8 = (bf16[256,256]{1,0:T(8,128)(2,1)S(1)}, bf16[256,256]{1,0:T(8,128)(2,1)}, u32[]{:S(2)}) copy-start(bf16[256,256]{1,0:T(8,128)(2,1)} %param.21) | copy-start | bytes 393220
  259.7 2.4 copy-start.10
  350.8 6.2 %copy-start.4 = (bf16[2,256,128]{2,1,0:T(8,128)(2,1)S(1)}, bf16[2,256,128]{2,1,0:T(8,128)(2,1)}, u32[]{:S(2)}) copy-start(bf16[2,256,128]{2,1,0:T(8,128)(2,1)} %param.15) | copy-start | bytes 393220
  350.8 6.2 %copy-start.7 = (bf16[1024,128]{1,0:T(8,128)(2,1)S(1)}, bf16[1024,128]{1,0:T(8,128)(2,1)}, u32[]{:S(2)}) copy-start(bf16[1024,128]{1,0:T(8,128)(2,1)} %param.23) | copy-start | bytes 786436
Sparse Core Ops, SparseCore 0:
  62.7 36.0 all-gather.3
  263.1 78.1 all-gather.5
where the time goes:
time: 368 us; the launch traced here: 365 us
  waiting for transfers between devices  124 us (34%)
  local copies, waits for them, and re-layouts  60.6 us (16%)
  matrix products  52.1 us (14%)
  blocking collectives  51.8 us (14%)
  Pallas kernels  30.7 us (8%)
  other arithmetic  16.8 us (5%)
  starting transfers between devices  14.8 us (4%)
  between operations  14.4 us (4%)
    all_gather x1, waiting for transfers between devices, shards(): piece = lax.all_gather(right, DAP, axis=1, tiled=True)  77.3 us
    all_gather x2, blocking collectives, stacked_from(): tiles = lax.all_gather(tiles, axes[k], axis=0, tiled=True)  51.8 us
    dot_general x8, Pallas kernels, one_head(): jnp.einsum('bij,bjd->bid', weights, vh, preferred_element_type=jnp.float32)  30.7 us
    all_gather x1, waiting for transfers between devices, stacked_from(): tiles = lax.all_gather(tiles, axes[k], axis=0, tiled=True)  27.3 us
    dynamic_slice x40, local copies, waits for them, and re-layouts, attend(): lax.map(one_head, (jnp.moveaxis(query, 2, 0), jnp.moveaxis(keys, 2, 0), j...  27.3 us
    all_to_all x1, waiting for transfers between devices, shards(): lax.all_to_all(homolog_later, DAP, split_axis=1, concat_axis=0, tiled=True)  18.9 us
    dynamic_update_slice x16, local copies, waits for them, and re-layouts, attend(): lax.map(one_head, (jnp.moveaxis(query, 2, 0), jnp.moveaxis(keys, 2, 0), j...  15 us
    dot_general x8, matrix products, one_head(): jnp.einsum('bij,bjd->bid', weights, vh, preferred_element_type=jnp.float32)  14.8 us
  transfers between devices with their start and end apart: 3, of which 3 were waited for; matrix products, arithmetic and copies ran while one was open for 2% of the time, Pallas kernels for 0%

commit v1 on v0

--- a/solution.py
+++ b/solution.py
@@ -113,7 +113,12 @@
     right = factors[..., FACTOR_FEATURES:].astype(jnp.bfloat16)
     total = left.shape[0]
     own_rows = left.shape[1]
-    piece = lax.all_gather(right, DAP, axis=1, tiled=True)
+    piece = jnp.concatenate(
+        jax.lax.all_to_all(
+            jnp.stack([right for _ in range(jax.lax.axis_size(DAP))], axis=0), DAP, 0, 0
+        ),
+        axis=1,
+    )
     outer = jnp.einsum("sic,sjd->ijcd", left, piece, preferred_element_type=jnp.float32) / total
     outer = outer.astype(jnp.bfloat16).reshape(
         own_rows, piece.shape[1], FACTOR_FEATURES * FACTOR_FEATURES

time: 368 us -> 531 us (1.44)
  the two profiles are of different devices: /device:TPU:513 before, /device:TPU:523 now
where the time goes in v1:
time: 531 us; the launch traced here: 529 us
  waiting for transfers between devices  272 us (51%)
  local copies, waits for them, and re-layouts  64.3 us (12%)
  matrix products  52.1 us (10%)
  blocking collectives  47.1 us (9%)
  Pallas kernels  30.7 us (6%)
  starting transfers between devices  30.5 us (6%)
  other arithmetic  16.8 us (3%)
  between operations  14.4 us (3%)
    all_to_all x1, waiting for transfers between devices, shards(): jax.lax.all_to_all(jnp.stack([right for _ in range(jax.lax.axis_size(DAP)...  228 us
    all_gather x2, blocking collectives, stacked_from(): tiles = lax.all_gather(tiles, axes[k], axis=0, tiled=True)  47.1 us
    dot_general x8, Pallas kernels, one_head(): jnp.einsum('bij,bjd->bid', weights, vh, preferred_element_type=jnp.float32)  30.7 us
    all_gather x1, waiting for transfers between devices, stacked_from(): tiles = lax.all_gather(tiles, axes[k], axis=0, tiled=True)  29.6 us
    dynamic_slice x40, local copies, waits for them, and re-layouts, attend(): lax.map(one_head, (jnp.moveaxis(query, 2, 0), jnp.moveaxis(keys, 2, 0), j...  27.3 us
    all_to_all x1, starting transfers between devices, shards(): lax.all_to_all(homolog_later, DAP, split_axis=1, concat_axis=0, tiled=True)  16.8 us
    dynamic_update_slice x16, local copies, waits for them, and re-layouts, attend(): lax.map(one_head, (jnp.moveaxis(query, 2, 0), jnp.moveaxis(keys, 2, 0), j...  15 us
    dot_general x8, matrix products, one_head(): jnp.einsum('bij,bjd->bid', weights, vh, preferred_element_type=jnp.float32)  14.8 us
  transfers between devices with their start and end apart: 3, of which 3 were waited for; matrix products, arithmetic and copies ran while one was open for 2% of the time, Pallas kernels for 0%

profile of v1, /device:TPU:523, one launch (start us, length us, event | category | flops | bytes accessed | tf_op | source)
XLA Modules:
  0.0 528.6 jit_solution(4830372524008518074)
XLA Ops:
  10.7 17.0 %all-gather = bf16[64,2,256]{2,0,1:T(8,128)(2,1)S(1)} all-gather(bf16[8,2,256]{2,0,1:T(8,128)(2,1)S(1)} %fusion.33), channel_id=2, replica_groups=mesh['groups'=2,'dap_0'=8,'dap_1'=8,'dap_2'=2] {'dap_0'}, dimensions={0}, use_global_device_ids=true | all-gather | bytes 73728 | tf_op jit(solution)/shard_map/all_gather | solution.py:23
  27.8 30.1 %all_gather.10 = bf16[64,8,2,256]{3,1,0,2:T(8,128)(2,1)} all-gather(bf16[8,8,2,256]{3,1,0,2:T(8,128)(2,1)S(1)} %bitcast.195), channel_id=1, replica_groups=mesh['groups'=2,'dap_0'=8,'dap_1'=8,'dap_2'=2] {'dap_1'}, dimensions={0}, use_global_device_ids=true | all-gather | bytes 589824 | tf_op jit(solution)/shard_map/all_gather | solution.py:23
  60.7 2.0 fusion.55
  66.8 29.6 %all-gather.3.cloned.1.call-done = bf16[128,8,2,256]{3,1,0,2:T(8,128)(2,1)} async-done(((bf16[64,8,2,256]{3,1,0,2:T(8,128)(2,1)}), bf16[128,8,2,256]{3,1,0,2:T(8,128)(2,1)}) %all-gather.3.cloned.1.call-update) | async-done | bytes 1048592 | tf_op jit(solution)/shard_map/all_gather | solution.py:23
  98.5 35.9 %while.20 = (s32[]{:T(128)}, f32[8,4,256,32]{2,3,0,1:T(8,128)}, bf16[8,4,256,32]{2,3,0,1:T(8,128)(2,1)}, bf16[8,4,256,32]{2,3,0,1:T(8,128)(2,1)}, bf16[8,256,256...) while((s32[]{:T(128)}, f32[8,4,256,32]{2,3,0,1:T(8,128)}, ...), condition=%wide.region_7.8_spmd, body=%wide.region_4.7_spmd.sunk | while | flops 52233728 | bytes 4533337 | solution.py:59
  101.2 1.9 fusion.102
  105.7 1.9 fusion.102
  110.2 1.9 fusion.102
  114.7 1.8 fusion.102
  119.2 1.8 fusion.102
  123.7 1.8 fusion.102
  128.1 1.8 fusion.102
  132.6 1.9 fusion.102
  134.5 1.8 fusion.50
  138.8 16.8 %all-to-all-start = ((bf16[4,256,256]{2,0,1:T(4,128)(2,1)}), bf16[4,256,256]{2,0,1:T(4,128)(2,1)S(1)}, u32[]{:S(2)}, u32[]{:S(2)}) async-start(bf16[4,256,256]{2,0,1:T(4,128)(2,1)} %copy.59), calls=%async_computation | async-start | bytes 1048576 | tf_op jit(solution)/shard_map/all_to_all | solution.py:97
  155.6 14.8 %all-to-all-done = bf16[4,256,256]{2,0,1:T(4,128)(2,1)S(1)} async-done(((bf16[4,256,256]{2,0,1:T(4,128)(2,1)}), bf16[4,256,256]{2,0,1:T(4,128)(2,1)S(1)}, u32[]{:S(2)}, u32[]{:S(2)}) %all-to-all-start) | async-done | bytes 524320 | tf_op jit(solution)/shard_map/all_to_all | solution.py:97
  180.0 2.1 slice_bitcast_fusion
  182.1 73.0 %while.21 = (s32[]{:T(128)}, f32[8,2,512,32]{2,3,0,1:T(8,128)}, bf16[8,2,512,32]{2,3,0,1:T(8,128)(2,1)S(1)}, bf16[8,2,512,32]{2,3,0,1:T(8,128)(2,1)}, bf16[8,2,512,32]{2,3,0,1:T(8,128)(2,1)S(1)}, /*index=5*/s32[]{:T(128)}) while((s32[]{:T(128)}, f32[8,2,512,32]{2,3,0,1:T(8,128)}, bf16[8,2,512,32]{2,3,0,1:T(8,128)(2,1)S(1)}, ...), condition=%wide.region_13.14_spmd, body=%wide.region_10.13_spmd.sunk | while | flops 67108864 | bytes 1507417 | solution.py:59
  185.5 3.8 dot_general.47
  194.6 3.8 dot_general.47
  203.8 3.8 dot_general.47
  212.9 3.8 dot_general.47
  222.0 3.8 dot_general.47
  231.1 3.8 dot_general.47
  240.3 3.8 dot_general.47
  249.4 3.8 dot_general.47
  255.1 1.8 fusion.51
  257.8 4.3 stack.2
  262.1 13.7 %all-to-all-start.1 = ((bf16[128,512,2,32]{1,3,2,0:T(8,128)(2,1)}), bf16[128,512,2,32]{1,3,2,0:T(8,128)(2,1)}, u32[]{:S(2)}, u32[]{:S(2)}) async-start(bf16[128,512,2,32]{1,3,2,0:T(8,128)(2,1)} %stack.2), calls=%async_computation.1 | async-start | bytes 16777216 | tf_op jit(solution)/shard_map/all_to_all | solution.py:117
  276.8 228.1 %all-to-all-done.1 = bf16[128,512,2,32]{1,3,2,0:T(8,128)(2,1)} async-done(((bf16[128,512,2,32]{1,3,2,0:T(8,128)(2,1)}), bf16[128,512,2,32]{1,3,2,0:T(8,128)(2,1)}, u32[]{:S(2)}, u32[]{:S(2)}) %all-to-all-start.1) | async-done | bytes 8388640 | tf_op jit(solution)/shard_map/all_to_all | solution.py:117
  504.9 9.4 %fusion.24 = bf16[2,256,32,32]{2,3,0,1:T(8,128)(2,1)} fusion(bf16[512,256,32,1]{0,2,3,1:T(8,128)(2,1)} %bitcast.52, bf16[512,2,64]{0,2,1:T(8,128)(2,1)S(1)} %convolution_convert_fusion), kind=kOutput, calls=%fused_computation.28 | convolution fusion | flops 537919488 | bytes 9502720 | tf_op jit(solution)/shard_map/sic,sjd->ijcd/dot_general | solution.py:122
  514.4 6.2 %copy.71 = bf16[2,256,32,32]{1,3,2,0:T(8,128)(2,1)S(1)} copy(bf16[2,256,32,32]{2,3,0,1:T(8,128)(2,1)} %fusion.24) | data formatting | bytes 2097152 | tf_op jit(solution)/shard_map/convert_element_type | solution.py:123
  (141 shorter events, 90.9 us)
Async XLA Ops:
  7.2 53.5 %copy-start = (bf16[256,1024]{1,0:T(8,128)(2,1)S(1)}, bf16[256,1024]{1,0:T(8,128)(2,1)}, u32[]{:S(2)}) copy-start(bf16[256,1024]{1,0:T(8,128)(2,1)} %param.18) | copy-start | bytes 1572868
  7.2 89.2 %all-gather.3.cloned.1.call-start = ((), (), s32[]{:S(2)}) async-start(), calls=%async_computation.2 | async-start | bytes 1572864 | tf_op jit(solution)/shard_map/all_gather | solution.py:23
  62.7 3.0 copy-start.2
  62.7 1.1 copy-start.6
  98.5 37.8 %copy-start.3 = (bf16[4,256,256]{2,1,0:T(8,128)(2,1)S(1)}, bf16[4,256,256]{2,1,0:T(8,128)(2,1)}, u32[]{:S(2)}) copy-start(bf16[4,256,256]{2,1,0:T(8,128)(2,1)} %param.14) | copy-start | bytes 1572868
  98.5 37.8 %copy-start.9 = (bf16[256,256]{1,0:T(8,128)(2,1)S(1)}, bf16[256,256]{1,0:T(8,128)(2,1)}, u32[]{:S(2)}) copy-start(bf16[256,256]{1,0:T(8,128)(2,1)} %param.19) | copy-start | bytes 393220
  138.8 36.0 %copy-start.5 = (bf16[256,1024]{1,0:T(8,128)(2,1)S(1)}, bf16[256,1024]{1,0:T(8,128)(2,1)}, u32[]{:S(2)}) copy-start(bf16[256,1024]{1,0:T(8,128)(2,1)} %param.20) | copy-start | bytes 1572868
  138.8 31.5 %all-to-all-start = ((bf16[4,256,256]{2,0,1:T(4,128)(2,1)}), bf16[4,256,256]{2,0,1:T(4,128)(2,1)S(1)}, u32[]{:S(2)}, u32[]{:S(2)}) async-start(bf16[4,256,256]{2,0,1:T(4,128)(2,1)} %copy.59), calls=%async_computation | async-start | bytes 1048576 | tf_op jit(solution)/shard_map/all_to_all | solution.py:97
  175.6 1.9 copy-start.1
  182.1 74.9 %copy-start.8 = (bf16[256,256]{1,0:T(8,128)(2,1)S(1)}, bf16[256,256]{1,0:T(8,128)(2,1)}, u32[]{:S(2)}) copy-start(bf16[256,256]{1,0:T(8,128)(2,1)} %param.21) | copy-start | bytes 393220
  255.1 2.4 copy-start.10
  262.1 242.9 %all-to-all-start.1 = ((bf16[128,512,2,32]{1,3,2,0:T(8,128)(2,1)}), bf16[128,512,2,32]{1,3,2,0:T(8,128)(2,1)}, u32[]{:S(2)}, u32[]{:S(2)}) async-start(bf16[128,512,2,32]{1,3,2,0:T(8,128)(2,1)} %stack.2), calls=%async_computation.1 | async-start | bytes 16777216 | tf_op jit(solution)/shard_map/all_to_all | solution.py:117
  514.4 6.2 %copy-start.4 = (bf16[2,256,128]{2,1,0:T(8,128)(2,1)S(1)}, bf16[2,256,128]{2,1,0:T(8,128)(2,1)}, u32[]{:S(2)}) copy-start(bf16[2,256,128]{2,1,0:T(8,128)(2,1)} %param.15) | copy-start | bytes 393220
  514.4 6.2 %copy-start.7 = (bf16[1024,128]{1,0:T(8,128)(2,1)S(1)}, bf16[1024,128]{1,0:T(8,128)(2,1)}, u32[]{:S(2)}) copy-start(bf16[1024,128]{1,0:T(8,128)(2,1)} %param.23) | copy-start | bytes 786436
Sparse Core Ops, SparseCore 0:
  58.0 38.2 all-gather.2
